TPU v7x, 32 devices: a whole 2x2x4 slice. The times are simulated.
32 devices in a mesh: dom: 4 (over y, core), rep: 8 (over z, x).
Axes of the slice: x: 2, y: 2, z: 4, core: 2. Of those that a mesh axis runs over, the one named last changes fastest.
Arguments:
- facts: float32 [131072, 256], P(('dom', 'rep')), may hold values from -6 to 6
- row_owner: int32 [131072, 1], P(('dom', 'rep')), may hold values from 0 to 3; in each aligned block of 4096 rows (0 to 4095, 4096 to 8191, ...) at most 2048 rows name the same one
- key_offset: int32 [131072], P(('dom', 'rep')), may hold values from 0 to 1023
Outputs:
- key_means: float32 [4096, 256], P(('dom', 'rep'))
- key_counts: float32 [4096], P(('dom', 'rep'))
Inputs may be any that keep to these rules, and one draw needn't show every extreme that they name: `row_owner`: in the rows of one device no key range is named by more than 2048 rows, a bound that some block reaches.
All inputs are finite; a program needn't handle non-finite values.
Results may differ from a plain program's by a relative error of at most 0.0003.
Values sent between devices are 32-bit elements; how exact they have to be, the bound alone decides.
A program may use at most 64 MiB of HBM per device.

v0:
```python
import jax
import jax.numpy as jnp
from jax import lax
from jax.sharding import PartitionSpec as P

KEYS = 4096


def block_table(offsets, high_part, low_part, start, key_step):
    wanted = start + jnp.arange(key_step, dtype=jnp.int32)
    onehot = (offsets[:, :, None] == wanted[None, None, :]).astype(jnp.bfloat16)
    upper = jnp.einsum("grk,grm->gkm", onehot, high_part, preferred_element_type=jnp.float32)
    lower = jnp.einsum("grk,grm->gkm", onehot, low_part, preferred_element_type=jnp.float32)
    return (upper + lower, jnp.sum(onehot, axis=1, dtype=jnp.float32))


def grouped_table(offsets, values, key_span):
    width = values.shape[-1]
    groups = offsets.shape[0]
    high_part = lax.optimization_barrier(values.astype(jnp.bfloat16))
    low_part = (values - high_part.astype(jnp.float32)).astype(jnp.bfloat16)
    key_step = min(512, key_span)
    blocks = key_span // key_step
    if blocks == 1:
        table_sums, table_counts = block_table(offsets, high_part, low_part, 0, key_step)
        return (
            table_sums.reshape(groups * key_span, width),
            table_counts.reshape(groups * key_span),
        )

    def one_block(block_index):
        return block_table(offsets, high_part, low_part, block_index * key_step, key_step)

    table_sums, table_counts = lax.map(one_block, jnp.arange(blocks, dtype=jnp.int32))
    table_sums = jnp.moveaxis(table_sums, 0, 1).reshape(groups * key_span, width)
    table_counts = jnp.moveaxis(table_counts, 0, 1).reshape(groups * key_span)
    return (table_sums, table_counts)


def bucket_rows(row_range, n_dom, capacity):
    rows_here = row_range.shape[0]
    range_hot = (row_range[:, None] == jnp.arange(n_dom, dtype=jnp.int32)[None, :]).astype(
        jnp.int32
    )
    before = jnp.cumsum(range_hot, axis=0) - range_hot
    slot_of = jnp.sum(range_hot * before, axis=1)
    position = row_range * capacity + slot_of
    empty = jnp.full((n_dom * capacity,), rows_here, jnp.int32)
    return empty.at[position].set(
        jnp.arange(rows_here, dtype=jnp.int32), unique_indices=True, mode="drop"
    )


def finish(table_sums, table_counts):
    return (table_sums / jnp.maximum(table_counts, 1.0)[:, None], table_counts)


def per_device(facts, row_owner, key_offset):
    row_range = row_owner[:, 0]
    n_dom = lax.axis_size("dom")
    key_span = KEYS // n_dom
    capacity = 2 * facts.shape[0] // n_dom
    measures = facts.shape[1]
    source = bucket_rows(row_range, n_dom, capacity)
    picked = jnp.take(facts, source, axis=0, mode="fill", fill_value=0.0)
    offsets = jnp.take(key_offset, source, axis=0, mode="fill", fill_value=-1)
    local_sums, local_counts = grouped_table(
        offsets.reshape(n_dom, capacity), picked.reshape(n_dom, capacity, measures), key_span
    )
    range_sums, range_counts = (
        lax.psum_scatter(local_sums, "dom", scatter_dimension=0, tiled=True),
        lax.psum_scatter(local_counts, "dom", scatter_dimension=0, tiled=True),
    )
    table_sums, table_counts = (
        lax.psum_scatter(range_sums, "rep", scatter_dimension=0, tiled=True),
        lax.psum_scatter(range_counts, "rep", scatter_dimension=0, tiled=True),
    )
    return finish(table_sums, table_counts)


def solution(mesh):
    placed = (P(("dom", "rep"), None), P(("dom", "rep"), None), P(("dom", "rep")))
    return jax.shard_map(
        per_device,
        mesh=mesh,
        in_specs=placed,
        out_specs=(P(("dom", "rep"), None), P(("dom", "rep"))),
        check_vma=False,
    )
```

profile of v0, /device:TPU:0, one launch (start us, length us, event | category | flops | bytes accessed | tf_op | source)
XLA Modules:
  0.0 269.2 jit_solution(16950049690493843657)
XLA Ops:
  7.2 0.0 copy-start
  7.2 0.0 reduce-scatter.3.cloned.1.call-start
  7.2 0.7 fusion.13
  8.0 1.1 reduce-window.6
  9.1 0.2 slice_reduce_fusion
  9.3 0.2 reduce-window.9
  9.5 0.1 add_bitcast_fusion
  9.6 0.8 fusion.12
  10.5 0.7 compare_select_fusion
  11.2 15.5 %scatter_custom_fusion = s32[8192]{0:T(1024)S(1)} fusion(s32[4096]{0:T(1024)S(1)} %bitcast.64, s32[4096]{0:T(1024)S(1)} %iota.19, s32[]{:T(128)} %constant.39.clone.1), kind=kCustom, calls=%fused_computation.34 | custom fusion | bytes 32772 | tf_op jit(solution)/shard_map/scatter | solution.py:49
  26.8 0.0 copy-done
  26.8 45.5 %gather_fusion = s32[8192]{0:T(1024)S(1)} fusion(s32[4096]{0:T(1024)S(1)} %copy-done, s32[8192]{0:T(1024)S(1)} %fusion.14), kind=kCustom, calls=%fused_computation | custom fusion | bytes 98304 | tf_op jit(solution)/shard_map/jit(_take)/gather | solution.py:66
  72.4 0.0 copy-start.6
  72.4 33.6 %gather_fusion.1 = f32[8192,256]{1,0:T(8,128)} fusion(f32[4096,256]{1,0:T(8,128)} %param.5, s32[8192]{0:T(1024)S(1)} %fusion.14), kind=kCustom, calls=%fused_computation.1 | custom fusion | bytes 16809984 | tf_op jit(solution)/shard_map/jit(_take)/gather | solution.py:65
  106.0 0.0 copy-start.1
  106.0 4.9 %select_convert_fusion = bf16[4,2048,256]{2,1,0:T(8,128)(2,1)S(1)} fusion(f32[4,2048,256]{2,1,0:T(8,128)} %bitcast.55, pred[4,2048]{1,0:T(4,128)(4,1)S(1)} %broadcast_in_dim.46), kind=kLoop, calls=%fused_computation.17 | loop fusion | flops 2097152 | bytes 12591104 | tf_op jit(solution)/shard_map/convert_element_type | solution.py:20
  110.9 1.0 copy-done.1
  111.9 0.0 copy-start.2
  111.9 4.1 %subtract_convert_fusion = bf16[4,2048,256]{2,1,0:T(8,128)(2,1)} fusion(bf16[4,2048,256]{2,1,0:T(8,128)(2,1)S(1)} %select_convert_fusion, f32[4,2048,256]{2,1,0:T(8,128)S(1)} %bitcast.56, pred[4,2048]{1,0:T(4,128)(4,1)S(1)} %broadcast_in_dim.46), kind=kLoop, calls=%fused_computation.16 | loop fusion | flops 8388608 | bytes 16785408 | tf_op jit(solution)/shard_map/convert_element_type | solution.py:21
  115.9 0.0 copy-done.2
  115.9 0.0 copy-done.6
  116.0 24.6 %while.13 = (s32[]{:T(128)}, f32[2,4,512,256]{3,2,1,0:T(8,128)}, f32[2,4,512]{2,1,0:T(4,128)S(1)}, s32[8192]{0:T(1024)}, s32[2]{0:T(128)S(1)}, /*index=5*/bf16[4...) while((s32[]{:T(128)}, f32[2,4,512,256]{3,2,1,0:T(8,128)}, ...), condition=%wide.wide.region_6.7_spmd, body=%wide.wide.region_4.6_spmd.sunk | while | flops 4320655872 | bytes 65143004 | solution.py:34
  116.0 0.6 dynamic_slice.6
  117.2 0.0 copy-start.3
  117.2 0.0 copy-start.4
  117.2 4.7 %fusion.33 = f32[4,512,256]{2,1,0:T(8,128)S(1)} fusion(bf16[4,2048,256]{2,1,0:T(8,128)(2,1)} %get-tuple-element.163, s32[4,2048]{1,0:T(4,128)S(1)} %get-tuple-element.164, s32[512]{0:T(512)S(1)} %iota_add_fusion.3), kind=kOutput, calls=%fused_computation.4.clone.clone.1 | convolution fusion | flops 2151677952 | bytes 6326272 | tf_op jit(solution)/shard_map/while/body/eval_jaxpr/grk,grm->gkm/dot_general | solution.py:13
  122.0 0.0 copy-done.3
  122.0 0.0 copy-done.4
  122.0 2.4 bitcast_dynamic-update-slice_fusion.6
  124.4 0.0 copy-start.5
  124.4 2.0 copy-done.5
  126.4 1.9 convert_reduce_fusion.3
  128.3 0.6 dynamic_slice.6
  129.5 0.0 copy-start.3
  129.5 0.0 copy-start.4
  129.6 4.7 %fusion.33 = f32[4,512,256]{2,1,0:T(8,128)S(1)} fusion(bf16[4,2048,256]{2,1,0:T(8,128)(2,1)} %get-tuple-element.163, s32[4,2048]{1,0:T(4,128)S(1)} %get-tuple-element.164, s32[512]{0:T(512)S(1)} %iota_add_fusion.3), kind=kOutput, calls=%fused_computation.4.clone.clone.1 | convolution fusion | flops 2151677952 | bytes 6326272 | tf_op jit(solution)/shard_map/while/body/eval_jaxpr/grk,grm->gkm/dot_general | solution.py:13
  134.3 0.0 copy-done.3
  134.3 0.0 copy-done.4
  134.3 2.4 bitcast_dynamic-update-slice_fusion.6
  136.7 0.0 copy-start.5
  136.8 2.0 copy-done.5
  138.7 1.9 convert_reduce_fusion.3
  140.6 4.4 %copy.8 = f32[4,2,512,256]{3,2,1,0:T(8,128)} copy(f32[4,2,512,256]{3,2,0,1:T(8,128)} %bitcast.58) | data formatting | bytes 8388608 | tf_op jit(solution)/shard_map/transpose | solution.py:35
  145.0 0.0 copy-start.8
  145.0 0.0 copy-start.7
  145.0 0.0 reduce-scatter.3.cloned.1.call-update
  145.1 0.0 reduce-scatter.5.cloned.1.call-start
  145.1 47.4 %reduce-scatter.3.cloned.1.call-done = f32[1024,256]{1,0:T(8,128)} async-done(((f32[4096,256]{1,0:T(8,128)}), f32[1024,256]{1,0:T(8,128)}) %reduce-scatter.3.cloned.1.call-update) | async-done | bytes 1048592 | tf_op jit(solution)/shard_map/reduce_scatter | solution.py:71
  192.5 0.0 reduce-scatter.5.cloned.1.call-update
  192.6 0.0 copy-done.8
  192.6 0.6 dynamic-slice
  193.2 0.0 copy-done.7
  193.2 0.6 dynamic-slice.2
  194.4 10.1 %all-reduce = f32[4096]{0:T(1024)S(1)} all-reduce(f32[4096]{0:T(1024)S(1)} %bitcast.61), channel_id=4, replica_groups=mesh['dom'=4,'rep'=8] {'dom'}, use_global_device_ids=true, to_apply=%region_9.10.clone | all-reduce | flops 4096 | bytes 32768
  205.2 21.7 %all-reduce.1 = f32[1024]{0:T(1024)S(1)} all-reduce(f32[1024]{0:T(1024)S(1)} %dynamic-slice.1), channel_id=5, replica_groups=mesh['dom'=4,'rep'=8] {'rep'}, use_global_device_ids=true, to_apply=%region_10.11.clone | all-reduce | flops 1024 | bytes 8192
  226.9 0.6 broadcast_maximum_fusion
  227.4 33.3 %reduce-scatter.5.cloned.1.call-done = f32[128,256]{1,0:T(8,128)} async-done(((f32[1024,256]{1,0:T(8,128)}), f32[128,256]{1,0:T(8,128)}) %reduce-scatter.5.cloned.1.call-update) | async-done | bytes 131088 | tf_op jit(solution)/shard_map/reduce_scatter | solution.py:75
  260.8 1.6 broadcast_divide_fusion
  (15 shorter events, 0.1 us)
Async XLA Ops:
  7.2 19.6 %copy-start = (s32[4096]{0:T(1024)S(1)}, s32[4096]{0:T(1024)}, u32[]{:S(2)}) copy-start(s32[4096]{0:T(1024)} %param.7) | copy-start | bytes 49156
  7.2 185.3 %reduce-scatter.3.cloned.1.call-start = ((), (), s32[]{:S(2)}) async-start(), calls=%async_computation.2 | async-start | bytes 5242880 | tf_op jit(solution)/shard_map/reduce_scatter | solution.py:71
  72.4 43.6 %copy-start.6 = (s32[8192]{0:T(1024)}, s32[8192]{0:T(1024)S(1)}, u32[]{:S(2)}) copy-start(s32[8192]{0:T(1024)S(1)} %get-tuple-element.140) | copy-start | bytes 98308
  106.0 5.9 %copy-start.1 = (f32[8192,256]{1,0:T(8,128)S(1)}, f32[8192,256]{1,0:T(8,128)}, u32[]{:S(2)}) copy-start(f32[8192,256]{1,0:T(8,128)} %gather_fusion.1) | copy-start | bytes 25165828
  111.9 4.1 %copy-start.2 = (bf16[4,2048,256]{2,1,0:T(8,128)(2,1)}, bf16[4,2048,256]{2,1,0:T(8,128)(2,1)S(1)}, u32[]{:S(2)}) copy-start(bf16[4,2048,256]{2,1,0:T(8,128)(2,1)S(1)} %select_convert_fusion) | copy-start | bytes 12582916
  117.2 4.7 %copy-start.3 = (bf16[4,2048,256]{2,1,0:T(8,128)(2,1)S(1)}, bf16[4,2048,256]{2,1,0:T(8,128)(2,1)}, u32[]{:S(2)}) copy-start(bf16[4,2048,256]{2,1,0:T(8,128)(2,1)} %get-tuple-element.162) | copy-start | bytes 12582916 | tf_op jit(solution)/shard_map/while
  117.2 4.7 %copy-start.4 = (f32[2,4,512,256]{3,2,1,0:T(8,128)S(1)}, f32[2,4,512,256]{3,2,1,0:T(8,128)}, u32[]{:S(2)}) copy-start(f32[2,4,512,256]{3,2,1,0:T(8,128)} %get-tuple-element.148) | copy-start | bytes 12582916 | tf_op jit(solution)/shard_map/while
  124.4 2.0 copy-start.5
  129.5 4.7 %copy-start.3 = (bf16[4,2048,256]{2,1,0:T(8,128)(2,1)S(1)}, bf16[4,2048,256]{2,1,0:T(8,128)(2,1)}, u32[]{:S(2)}) copy-start(bf16[4,2048,256]{2,1,0:T(8,128)(2,1)} %get-tuple-element.162) | copy-start | bytes 12582916 | tf_op jit(solution)/shard_map/while
  129.5 4.7 %copy-start.4 = (f32[2,4,512,256]{3,2,1,0:T(8,128)S(1)}, f32[2,4,512,256]{3,2,1,0:T(8,128)}, u32[]{:S(2)}) copy-start(f32[2,4,512,256]{3,2,1,0:T(8,128)} %get-tuple-element.148) | copy-start | bytes 12582916 | tf_op jit(solution)/shard_map/while
  136.7 2.0 copy-start.5
  145.0 47.5 %copy-start.8 = (u32[32]{0:T(128)S(1)}, u32[32]{0:T(128)}, u32[]{:S(2)}) copy-start(u32[32]{0:T(128)} %constant.60) | copy-start | bytes 388
  145.0 48.1 %copy-start.7 = (u32[32]{0:T(128)S(1)}, u32[32]{0:T(128)}, u32[]{:S(2)}) copy-start(u32[32]{0:T(128)} %constant.64) | copy-start | bytes 388
  145.1 115.7 %reduce-scatter.5.cloned.1.call-start = ((), (), s32[]{:S(2)}) async-start(), calls=%async_computation.3 | async-start | bytes 1179648 | tf_op jit(solution)/shard_map/reduce_scatter | solution.py:75
Sparse Core Ops, SparseCore 0:
  145.2 47.2 reduce-scatter.2
  195.9 64.8 reduce-scatter.4
where the time goes:
time: 270 us; the launch traced here: 269 us
  local copies, waits for them, and re-layouts  107 us (40%)
  waiting for transfers between devices  80.7 us (30%)
  blocking collectives  31.8 us (12%)
  other arithmetic  18.7 us (7%)
  between operations  15.5 us (6%)
  matrix products  14.3 us (5%)
    reduce_scatter x1, waiting for transfers between devices, per_device(): lax.psum_scatter(local_sums, 'dom', scatter_dimension=0, tiled=True)  47.4 us
    gather x1, local copies, waits for them, and re-layouts, per_device(): offsets = jnp.take(key_offset, source, axis=0, mode='fill', fill_value=-1)  45.5 us
    gather x1, local copies, waits for them, and re-layouts, per_device(): picked = jnp.take(facts, source, axis=0, mode='fill', fill_value=0.0)  33.6 us
    reduce_scatter x1, waiting for transfers between devices, per_device(): lax.psum_scatter(range_sums, 'rep', scatter_dimension=0, tiled=True)  33.3 us
    unnamed x2, blocking collectives  31.8 us
    scatter x1, local copies, waits for them, and re-layouts, bucket_rows(): empty.at[position]  15.5 us
    dot_general x2, matrix products, block_table(): jnp.einsum('grk,grm->gkm', onehot, low_part, preferred_element_type=jnp.f...  9.42 us
  transfers between devices with their start and end apart: 2, of which 2 were waited for; matrix products, arithmetic and copies ran while one was open for 1% of the time, Pallas kernels for 0%

commit v1 on v0

v1 whole, which is shorter than its diff:
```python
import functools

import jax
import jax.numpy as jnp
from jax import lax
from jax.experimental import pallas as pl
from jax.experimental.pallas import tpu as pltpu
from jax.sharding import PartitionSpec as P

KEYS = 4096
MESH = pl.DeviceIdType.MESH
F32 = jnp.float32
BF16 = jnp.bfloat16


def flip(index, bits):
    at = 1
    while at <= bits:
        if bits & at:
            index = index + at * (1 - 2 * ((index // at) % 2))
        at *= 2
    return index


def kernel(D, Z, hb, rows, M, chunk, lab_ref, crow_ref, ccol_ref, facts_ref, out_ref, cout_ref,
           fbuf, X, sendC1, sendC2, recvC1, recvC2, acc1, acc2,
           rA1, rB1, rA2, rB2, rZ,
           c0, cS, cR, cD, cX, cXr, cZ, cZr, fsem,
           sC1, tC1, sC2, tC2, sA1, tA1, sB1, tB1, sA2, tA2, sB2, tB2, sZ, tZ,
           scC, tcC, scD, tcD, scX, tcX, scZ, tcZ):
    me_d, me_r = lax.axis_index("dom"), lax.axis_index("rep")
    T1, T2 = (3 * D - 2) * hb, (D + 2) * hb
    stage = 4 * D * hb
    core = (flip(me_d, 1), me_r)
    dpeer = [None] + [(flip(me_d, 2 * d), me_r) for d in range(1, D)]
    xpeer = (me_d, flip(me_r, 1))
    zpeer = [None] + [(me_d, flip(me_r, 2 * z)) for z in range(1, Z)]
    peers = [core] + dpeer[1:] + [xpeer] + zpeer[1:]

    nchunks = rows // chunk
    loads = [
        pltpu.make_async_copy(
            facts_ref.at[pl.ds(k * chunk, chunk)], fbuf.at[pl.ds(k * chunk, chunk)], fsem.at[k]
        )
        for k in range(nchunks)
    ]
    for ld in loads:
        ld.start()
    barrier = pltpu.get_barrier_semaphore()
    for p in peers:
        pl.semaphore_signal(barrier, inc=1, device_id=p, device_id_type=MESH)

    def rcopy(src, dst, s, t, dev):
        return pltpu.make_async_remote_copy(
            src_ref=src, dst_ref=dst, send_sem=s, recv_sem=t, device_id=dev, device_id_type=MESH
        )

    nrow = 4 * D * Z
    kpd = 2 * hb
    hot_r = jnp.where(lax.broadcasted_iota(jnp.int32, (nrow, rows), 0) == crow_ref[...], 1.0, 0.0).astype(BF16)
    hot_c = jnp.where(lax.broadcasted_iota(jnp.int32, (kpd, rows), 0) == ccol_ref[...], 1.0, 0.0).astype(BF16)
    cnt = lax.dot_general(hot_r, hot_c, (((1,), (1,)), ((), ())), preferred_element_type=F32)
    half = nrow // 2
    for d in range(D):
        c0[d] = cnt[d * 2 * Z:(d + 1) * 2 * Z]
        cS[d] = cnt[half + d * 2 * Z:half + (d + 1) * 2 * Z]

    for k in range(nchunks):
        loads[k].wait()

        @pl.loop(0, chunk // 256)
        def _(j):
            at = pl.multiple_of(k * chunk + j * 256, 256)
            v = fbuf[pl.ds(at, 256), :]
            hi = v.astype(BF16)
            X[pl.ds(at, 256), 0:M] = hi
            X[pl.ds(at, 256), M:2 * M] = (v - hi.astype(F32)).astype(BF16)

    pl.semaphore_wait(barrier, len(peers))
    cc = rcopy(cS, cR, scC, tcC, core)
    cc.start()

    def tile(start, size):
        rel = lab_ref[...] - start
        total = None
        for k in range(nchunks):
            part = rel[:, k * chunk:(k + 1) * chunk]
            hot = jnp.where(lax.broadcasted_iota(jnp.int32, (size, chunk), 0) == part, 1.0, 0.0).astype(BF16)
            o = jnp.dot(hot, X[k * chunk:(k + 1) * chunk, :], preferred_element_type=F32)
            total = o if total is None else total + o
        return total[:, 0:M] + total[:, M:2 * M]

    def C1(i):
        return rcopy(sendC1.at[i], recvC1.at[i], sC1.at[i], tC1.at[i], core)

    def C2(i):
        return rcopy(sendC2.at[i], recvC2.at[i], sC2.at[i], tC2.at[i], core)

    def A1(i, d):
        return rcopy(acc1.at[i, pl.ds(2 * (d - 1) * hb, 2 * hb)], rA1.at[i, d - 1],
                     sA1.at[i, d - 1], tA1.at[i, d - 1], dpeer[d])

    def B1(i):
        return rcopy(acc1.at[i, pl.ds(2 * (D - 1) * hb, D * hb)], rB1.at[i], sB1.at[i], tB1.at[i], xpeer)

    def A2(i):
        return rcopy(acc2.at[i, pl.ds(0, hb)], rA2.at[i], sA2.at[i], tA2.at[i], xpeer)

    def B2(i, d):
        return rcopy(acc2.at[i, pl.ds(d * hb, hb)], rB2.at[i, d - 1], sB2.at[i, d - 1], tB2.at[i, d - 1], dpeer[d])

    def ZC(i, z):
        return rcopy(acc2.at[i, pl.ds(D * hb, 2 * hb)], rZ.at[i], sZ.at[i], tZ.at[i], zpeer[z])

    def phase1(i):
        C1(i).wait_recv()
        acc1[i] = acc1[i] + recvC1[i]
        for d in range(1, D):
            A1(i, d).start()
        B1(i).start()

    def core2(i):
        C2(i).wait_recv()
        acc2[i] = acc2[i] + recvC2[i]

    def phase2(i):
        x0 = pl.ds(D * hb, hb)
        for d in range(1, D):
            A1(i, d).wait_recv()
            acc2[i, 0:hb] = acc2[i, 0:hb] + rA1[i, d - 1, hb:2 * hb]
        A2(i).start()
        B1(i).wait_recv()
        for d in range(1, D):
            acc2[i, d * hb:(d + 1) * hb] = acc2[i, d * hb:(d + 1) * hb] + rB1[i, d * hb:(d + 1) * hb]
            B2(i, d).start()
        extra = rA1[i, 0, 0:hb]
        for d in range(2, D):
            extra = extra + rA1[i, d - 1, 0:hb]
        acc2[i, x0] = acc2[i, x0] + extra
        b0 = pl.ds((D + 1) * hb, hb)
        acc2[i, b0] = acc2[i, b0] + rB1[i, 0:hb]

    def phase3(i):
        x0 = pl.ds(D * hb, hb)
        b0 = pl.ds((D + 1) * hb, hb)
        A2(i).wait_recv()
        acc2[i, x0] = acc2[i, x0] + rA2[i]
        for d in range(1, D):
            B2(i, d).wait_recv()
            acc2[i, b0] = acc2[i, b0] + rB2[i, d - 1]
        for z in range(1, Z):
            @pl.when(i == Z - 1 - z)
            def _():
                ZC(i, z).start()

    def DC(d):
        return rcopy(c0.at[d], cD.at[d - 1], scD.at[d - 1], tcD.at[d - 1], dpeer[d])

    def XC():
        return rcopy(cX, cXr, scX, tcX, xpeer)

    def ZCc(z):
        return rcopy(cZ, cZr.at[z - 1], scZ.at[z - 1], tcZ.at[z - 1], zpeer[z])

    def count_step(i):
        @pl.when(i == 0)
        def _():
            cc.wait_recv()
            for d in range(D):
                c0[d] = c0[d] + cR[d]
            for d in range(1, D):
                DC(d).start()

        @pl.when(i == 1)
        def _():
            v = c0[0]
            for d in range(1, D):
                DC(d).wait_recv()
                v = v + cD[d - 1]
            cX[...] = v
            XC().start()

        @pl.when(i == 2)
        def _():
            XC().wait_recv()
            cZ[...] = cX[0:Z] + cXr[Z:2 * Z]
            for z in range(1, Z):
                ZCc(z).start()

    @pl.loop(0, Z + 3)
    def _(i):
        @pl.when(i < Z)
        def _():
            base = i * 2 * stage
            sendC1[i] = tile(base + stage, T1)
            C1(i).start()

        @pl.when((i >= 1) & (i <= Z))
        def _():
            core2(i - 1)

        @pl.when((i >= 2) & (i <= Z + 1))
        def _():
            phase2(i - 2)

        @pl.when(i < Z)
        def _():
            base = i * 2 * stage
            acc1[i] = tile(base, T1)
            count_step(i)
            sendC2[i] = tile(base + stage + T1, T2)
            C2(i).start()
            phase1(i)

        @pl.when(i >= 3)
        def _():
            phase3(i - 3)

        @pl.when(i < Z)
        def _():
            acc2[i] = tile(i * 2 * stage + T1, T2)

    cf = cZ[0:1, :]
    for z in range(1, Z):
        ZCc(z).wait_recv()
        cf = cf + cZr[z - 1, z:z + 1, :]
    cout_ref[...] = cf
    spread = jnp.broadcast_to(jnp.maximum(cf, 1.0), (kpd, kpd))
    eye = lax.broadcasted_iota(jnp.int32, (kpd, kpd), 0) == lax.broadcasted_iota(jnp.int32, (kpd, kpd), 1)
    col = jnp.sum(jnp.where(eye, spread, 0.0), axis=1, keepdims=True)
    tot = acc2[Z - 1, D * hb:(D + 2) * hb]
    for i in range(Z - 1):
        ZC(i, Z - 1 - i).wait_recv()
        tot = tot + rZ[i]
    out_ref[...] = tot / col

    cc.wait_send()
    for d in range(1, D):
        DC(d).wait_send()
    XC().wait_send()
    for z in range(1, Z):
        ZCc(z).wait_send()
        ZC(Z - 1 - z, z).wait_send()

    @pl.loop(0, Z)
    def _(i):
        C1(i).wait_send()
        C2(i).wait_send()
        for d in range(1, D):
            A1(i, d).wait_send()
            B2(i, d).wait_send()
        B1(i).wait_send()
        A2(i).wait_send()


def per_device(facts, row_owner, key_offset):
    n_dom, n_rep = lax.axis_size("dom"), lax.axis_size("rep")
    rows, M = facts.shape
    D, Z = n_dom // 2, n_rep // 2
    kpd = KEYS // (n_dom * n_rep)
    hb = kpd // 2
    T1, T2 = (3 * D - 2) * hb, (D + 2) * hb
    owner = row_owner[:, 0]
    rel = owner ^ lax.axis_index("dom")
    dc, d = rel & 1, rel >> 1
    i = key_offset % kpd
    rr = (key_offset // kpd) ^ lax.axis_index("rep")
    x, z = rr & 1, rr >> 1
    h, ii = i // hb, i % hb
    blk_a = jnp.where(d > 0, 2 * (d - 1) + x, jnp.where(x > 0, 3 * D - 2, 4 * D - 2))
    blk_b = jnp.where(x > 0, 2 * (D - 1) + d, jnp.where(d > 0, 3 * D - 2 + d, 4 * D - 1))
    blk = jnp.where(h > 0, blk_b, blk_a)
    label = (((Z - 1 - z) * 2 + dc) * (4 * D) + blk) * hb + ii
    crow = ((dc * D + d) * 2 + x) * Z + z
    chunk = min(1024, rows)

    def vm(*shape, dtype=F32):
        return pltpu.VMEM(shape, dtype)

    def dma(*shape):
        return [pltpu.SemaphoreType.DMA(shape)] * 2 if shape else [pltpu.SemaphoreType.DMA] * 2

    scratch = [
        vm(rows, M), vm(rows, 2 * M, dtype=BF16),
        vm(Z, T1, M), vm(Z, T2, M), vm(Z, T1, M), vm(Z, T2, M), vm(Z, T1, M), vm(Z, T2, M),
        vm(Z, D - 1, 2 * hb, M), vm(Z, D * hb, M), vm(Z, hb, M), vm(Z, D - 1, hb, M), vm(Z - 1, 2 * hb, M),
        vm(D, 2 * Z, kpd), vm(D, 2 * Z, kpd), vm(D, 2 * Z, kpd), vm(D - 1, 2 * Z, kpd),
        vm(2 * Z, kpd), vm(2 * Z, kpd), vm(Z, kpd), vm(Z - 1, Z, kpd),
        pltpu.SemaphoreType.DMA((rows // chunk,)),
        *dma(Z), *dma(Z), *dma(Z, D - 1), *dma(Z), *dma(Z), *dma(Z, D - 1), *dma(Z - 1),
        *dma(), *dma(D - 1), *dma(), *dma(Z - 1),
    ]
    vmem = pl.BlockSpec(memory_space=pltpu.VMEM)
    means, counts = pl.pallas_call(
        functools.partial(kernel, D, Z, hb, rows, M, chunk),
        out_shape=(jax.ShapeDtypeStruct((kpd, M), F32), jax.ShapeDtypeStruct((1, kpd), F32)),
        in_specs=[vmem, vmem, vmem, pl.BlockSpec(memory_space=pl.ANY)],
        out_specs=(vmem, vmem),
        scratch_shapes=scratch,
        compiler_params=pltpu.CompilerParams(
            collective_id=0, has_side_effects=True, vmem_limit_bytes=50 * 1024 * 1024
        ),
    )(label[None, :], crow[None, :], i[None, :], facts)
    return means, counts.reshape(kpd)


def solution(mesh):
    placed = (P(("dom", "rep"), None), P(("dom", "rep"), None), P(("dom", "rep")))
    return jax.shard_map(
        per_device,
        mesh=mesh,
        in_specs=placed,
        out_specs=(P(("dom", "rep"), None), P(("dom", "rep"))),
        check_vma=False,
    )
```

time: 270 us -> 50.4 us (0.19)
  local copies, waits for them, and re-layouts: 107 us -> 1.17 us
  waiting for transfers between devices: 80.7 us -> 0 us
  Pallas kernels: 0 us -> 46.8 us
  blocking collectives: 31.8 us -> 0 us
  other arithmetic: 18.7 us -> 1.52 us
  between operations: 15.5 us -> 0.65 us
  matrix products: 14.3 us -> 0 us
    reduce_scatter x2 -> x0, waiting for transfers between devices: 80.7 us -> none  [the longest x1 47.4 us: per_device(): lax.psum_scatter(local_sums, 'dom', scatter_dimension=0, tiled=True)]
    gather x2 -> x0, local copies, waits for them, and re-layouts: 79.1 us -> none  [the longest x1 45.5 us: per_device(): offsets = jnp.take(key_offset, source, axis=0, mode='fill', fill_value=-1)]
    pallas_call x0 -> x1, Pallas kernels: none -> 46.8 us  [per_device(): pl.pallas_call(functools.partial(kernel, D, Z, hb, rows, M, chunk), out_s...]
    unnamed x2 -> x0, blocking collectives: 31.8 us -> none
    scatter x1 -> x0, local copies, waits for them, and re-layouts: 15.5 us -> none  [bucket_rows(): empty.at[position]]
    dot_general x4 -> x0, matrix products: 14.3 us -> none  [the longest x2 9.42 us: block_table(): jnp.einsum('grk,grm->gkm', onehot, low_part, preferred_element_type=jnp.f...]
    convert_element_type x3 -> x0, other arithmetic: 9.71 us -> none  [the longest x1 4.91 us: grouped_table(): high_part = lax.optimization_barrier(values.astype(jnp.bfloat16))]
    reduce_sum x3 -> x0, other arithmetic: 4.55 us -> none  [the longest x2 3.74 us: block_table(): return (upper + lower, jnp.sum(onehot, axis=1, dtype=jnp.float32))]
  transfers between devices with their start and end apart: 2 -> 0, of which waited for: 2 -> 0; matrix products, arithmetic and copies ran while one was open for 1% -> 0% of each run, Pallas kernels for 0% -> 0%
where the time goes in v1:
time: 50.4 us; the launch traced here: 50.1 us
  Pallas kernels  46.8 us (93%)
  other arithmetic  1.52 us (3%)
  local copies, waits for them, and re-layouts  1.17 us (2%)
  between operations  0.65 us (1%)
    pallas_call x1, Pallas kernels, per_device(): pl.pallas_call(functools.partial(kernel, D, Z, hb, rows, M, chunk), out_s...  46.8 us
    unnamed x2, local copies, waits for them, and re-layouts  1.17 us

profile of v1, /device:TPU:0, one launch (start us, length us, event | category | flops | bytes accessed | tf_op | source)
XLA Modules:
  0.0 50.1 jit_solution(86506155289073508)
XLA Ops:
  0.6 0.7 %xor_and_fusion = (s32[4096,1]{0,1:T(1,128)S(1)}, s32[4096,1]{0,1:T(1,128)S(1)}) fusion(s32[4096,1]{0,1:T(1,128)} %param.4, s32[]{:T(128)S(6)} %axis_index.25), kind=kLoop, calls=%fused_computation.21 | loop fusion | flops 12288 | bytes 49156 | tf_op jit(solution)/shard_map/and | solution.py:265
  1.4 0.8 %multiply_add_fusion = (s32[4096]{0:T(1024)S(1)}, s32[4096]{0:T(1024)S(1)}, s32[4096]{0:T(1024)S(1)}) fusion(s32[4096]{0:T(1024)S(1)} %bitcast.11, s32[4096]{0:T(1024)S(1)} %bitcast.10, s32[]{:T(128)S(6)} %axis_index.22, s32[4096]{0:T(1024)} %param.5), kind=kLoop, calls=%fused_computation.13 | loop fusion | flops 274432 | bytes 98308 | tf_op jit(solution)/shard_map/add | solution.py:274
  2.2 46.8 %shard_map.50 = (f32[128,256]{1,0:T(8,128)S(1)}, f32[1,128]{1,0:T(1,128)S(1)}) custom-call(s32[1,4096]{1,0:T(1,128)S(1)} %bitcast.7, s32[1,4096]{1,0:T(1,128)S(1)} %bitcast.6, s32[1,4096]{1,0:T(1,128)S(1)} %bitcast.8, f32[4096,256]{1,0:T(8,128)} %facts_ref.1), custom_call_target="tpu_custom_call" | custom-call | tf_op jit(solution)/shard_map/pallas_call | solution.py:294
  48.9 0.7 %copy.7 = f32[128,256]{1,0:T(8,128)} copy(f32[128,256]{1,0:T(8,128)S(1)} %get-tuple-element.13) | data formatting | bytes 262144
  49.6 0.5 %copy.8 = f32[128]{0:T(128)} copy(f32[128]{0:T(128)S(1)} %bitcast.9) | data formatting | bytes 1024

commit v2 on v1

v2 whole, which is shorter than its diff:
```python
import functools

import jax
import jax.numpy as jnp
from jax import lax
from jax.experimental import pallas as pl
from jax.experimental.pallas import tpu as pltpu
from jax.sharding import PartitionSpec as P

KEYS = 4096
MESH = pl.DeviceIdType.MESH
F32 = jnp.float32
BF16 = jnp.bfloat16


def flip(index, bits):
    at = 1
    while at <= bits:
        if bits & at:
            index = index + at * (1 - 2 * ((index // at) % 2))
        at *= 2
    return index


def kernel(D, Z, hb, rows, M, chunk, owner_hbm, offset_hbm, facts_ref, out_ref, cout_ref,
           owner_ref, offset_ref, lab_ref, fbuf, high, low, tab, recvC1, recvC2,
           rA1, rB1, rA2, rB2, rZ,
           c0, cS, cR, cD, cX, cXr, cZ, cZr, fsem, isem,
           sC1, tC1, sC2, tC2, sA1, tA1, sB1, tB1, sA2, tA2, sB2, tB2, sZ, tZ,
           scC, tcC, scD, tcD, scX, tcX, scZ, tcZ):
    me_d, me_r = lax.axis_index("dom"), lax.axis_index("rep")
    T1, T2 = (3 * D - 2) * hb, (D + 2) * hb
    stage = 4 * D * hb
    core = (flip(me_d, 1), me_r)
    dpeer = [None] + [(flip(me_d, 2 * d), me_r) for d in range(1, D)]
    xpeer = (me_d, flip(me_r, 1))
    zpeer = [None] + [(me_d, flip(me_r, 2 * z)) for z in range(1, Z)]
    peers = [core] + dpeer[1:] + [xpeer] + zpeer[1:]

    nchunks = rows // chunk
    loads = [
        pltpu.make_async_copy(
            facts_ref.at[pl.ds(k * chunk, chunk)], fbuf.at[pl.ds(k * chunk, chunk)], fsem.at[k]
        )
        for k in range(nchunks)
    ]
    ints = [
        pltpu.make_async_copy(owner_hbm, owner_ref, isem.at[0]),
        pltpu.make_async_copy(offset_hbm, offset_ref, isem.at[1]),
    ]
    for ld in ints + loads:
        ld.start()
    barrier = pltpu.get_barrier_semaphore()
    for p in peers:
        pl.semaphore_signal(barrier, inc=1, device_id=p, device_id_type=MESH)

    def rcopy(src, dst, s, t, dev):
        return pltpu.make_async_remote_copy(
            src_ref=src, dst_ref=dst, send_sem=s, recv_sem=t, device_id=dev, device_id_type=MESH
        )

    nrow = 4 * D * Z
    kpd = 2 * hb
    for ld in ints:
        ld.wait()
    rel = owner_ref[...] ^ me_d
    dc, d = rel & 1, rel >> 1
    offset = offset_ref[...]
    i = offset & (kpd - 1)
    rr = (offset >> (kpd.bit_length() - 1)) ^ me_r
    x, z = rr & 1, rr >> 1
    ii = i & (hb - 1)
    blk_a = jnp.where(d > 0, 2 * (d - 1) + x, jnp.where(x > 0, 3 * D - 2, 4 * D - 2))
    blk_b = jnp.where(x > 0, 2 * (D - 1) + d, jnp.where(d > 0, 3 * D - 2 + d, 4 * D - 1))
    blk = jnp.where(i >= hb, blk_b, blk_a)
    lab_ref[...] = (((Z - 1 - z) * 2 + dc) * (4 * D) + blk) * hb + ii
    crow = ((dc * D + d) * 2 + x) * Z + z
    hot_r = jnp.where(lax.broadcasted_iota(jnp.int32, (nrow, rows), 0) == crow, 1.0, 0.0).astype(BF16)
    hot_c = jnp.where(lax.broadcasted_iota(jnp.int32, (kpd, rows), 0) == i, 1.0, 0.0).astype(BF16)
    cnt = lax.dot_general(hot_r, hot_c, (((1,), (1,)), ((), ())), preferred_element_type=F32)
    half = nrow // 2
    for d in range(D):
        c0[d] = cnt[d * 2 * Z:(d + 1) * 2 * Z]
        cS[d] = cnt[half + d * 2 * Z:half + (d + 1) * 2 * Z]

    for k in range(nchunks):
        loads[k].wait()

        @pl.loop(0, chunk // 256)
        def _(j):
            at = pl.multiple_of(k * chunk + j * 256, 256)
            v = fbuf[pl.ds(at, 256), :]
            hi = v.astype(BF16)
            high[pl.ds(at, 256), :] = hi
            low[pl.ds(at, 256), :] = (v - hi.astype(F32)).astype(BF16)

    pl.semaphore_wait(barrier, len(peers))
    cc = rcopy(cS, cR, scC, tcC, core)
    cc.start()

    def tile(start, size):
        rel = lab_ref[...] - start
        total = None
        for k in range(nchunks):
            part = rel[:, k * chunk:(k + 1) * chunk]
            hot = jnp.where(lax.broadcasted_iota(jnp.int32, (size, chunk), 0) == part, 1.0, 0.0).astype(BF16)
            at = slice(k * chunk, (k + 1) * chunk)
            o = jnp.dot(hot, high[at, :], preferred_element_type=F32) + jnp.dot(
                hot, low[at, :], preferred_element_type=F32
            )
            total = o if total is None else total + o
        return total

    def C1(i):
        return rcopy(tab.at[4 * i, pl.ds(0, T1)], recvC1.at[i], sC1.at[i], tC1.at[i], core)

    def C2(i):
        return rcopy(tab.at[4 * i + 2, pl.ds(0, T2)], recvC2.at[i], sC2.at[i], tC2.at[i], core)

    def A1(i, d):
        return rcopy(tab.at[4 * i + 1, pl.ds(2 * (d - 1) * hb, 2 * hb)], rA1.at[i, d - 1],
                     sA1.at[i, d - 1], tA1.at[i, d - 1], dpeer[d])

    def B1(i):
        return rcopy(tab.at[4 * i + 1, pl.ds(2 * (D - 1) * hb, D * hb)], rB1.at[i], sB1.at[i], tB1.at[i], xpeer)

    def A2(i):
        return rcopy(tab.at[4 * i + 3, pl.ds(0, hb)], rA2.at[i], sA2.at[i], tA2.at[i], xpeer)

    def B2(i, d):
        return rcopy(tab.at[4 * i + 3, pl.ds(d * hb, hb)], rB2.at[i, d - 1], sB2.at[i, d - 1], tB2.at[i, d - 1], dpeer[d])

    def ZC(i, z):
        return rcopy(tab.at[4 * i + 3, pl.ds(D * hb, 2 * hb)], rZ.at[i], sZ.at[i], tZ.at[i], zpeer[z])

    def phase1(i):
        C1(i).wait_recv()
        tab[4 * i + 1, 0:T1] = tab[4 * i + 1, 0:T1] + recvC1[i]
        for d in range(1, D):
            A1(i, d).start()
        B1(i).start()

    def core2(i):
        C2(i).wait_recv()
        tab[4 * i + 3, 0:T2] = tab[4 * i + 3, 0:T2] + recvC2[i]

    def phase2(i):
        x0 = pl.ds(D * hb, hb)
        for d in range(1, D):
            A1(i, d).wait_recv()
            tab[4 * i + 3, 0:hb] = tab[4 * i + 3, 0:hb] + rA1[i, d - 1, hb:2 * hb]
        A2(i).start()
        B1(i).wait_recv()
        for d in range(1, D):
            tab[4 * i + 3, d * hb:(d + 1) * hb] = tab[4 * i + 3, d * hb:(d + 1) * hb] + rB1[i, d * hb:(d + 1) * hb]
            B2(i, d).start()
        extra = rA1[i, 0, 0:hb]
        for d in range(2, D):
            extra = extra + rA1[i, d - 1, 0:hb]
        tab[4 * i + 3, x0] = tab[4 * i + 3, x0] + extra
        b0 = pl.ds((D + 1) * hb, hb)
        tab[4 * i + 3, b0] = tab[4 * i + 3, b0] + rB1[i, 0:hb]

    def phase3(i):
        x0 = pl.ds(D * hb, hb)
        b0 = pl.ds((D + 1) * hb, hb)
        A2(i).wait_recv()
        tab[4 * i + 3, x0] = tab[4 * i + 3, x0] + rA2[i]
        for d in range(1, D):
            B2(i, d).wait_recv()
            tab[4 * i + 3, b0] = tab[4 * i + 3, b0] + rB2[i, d - 1]
        for z in range(1, Z):
            if isinstance(i, int):
                if i == Z - 1 - z:
                    ZC(i, z).start()
                continue

            @pl.when(i == Z - 1 - z)
            def _():
                ZC(i, z).start()

    def DC(d):
        return rcopy(c0.at[d], cD.at[d - 1], scD.at[d - 1], tcD.at[d - 1], dpeer[d])

    def XC():
        return rcopy(cX, cXr, scX, tcX, xpeer)

    def ZCc(z):
        return rcopy(cZ, cZr.at[z - 1], scZ.at[z - 1], tcZ.at[z - 1], zpeer[z])

    def count_step(i):
        @pl.when(i == 0)
        def _():
            cc.wait_recv()
            for d in range(D):
                c0[d] = c0[d] + cR[d]
            for d in range(1, D):
                DC(d).start()

        @pl.when(i == 1)
        def _():
            v = c0[0]
            for d in range(1, D):
                DC(d).wait_recv()
                v = v + cD[d - 1]
            cX[...] = v
            XC().start()

        @pl.when(i == 2)
        def _():
            XC().wait_recv()
            cZ[...] = cX[0:Z] + cXr[Z:2 * Z]
            for z in range(1, Z):
                ZCc(z).start()

    @pl.loop(0, 4 * Z)
    def _(t):
        i, j = t // 4, t % 4
        tab[t] = tile((2 * i + 1 - j % 2) * stage + (j // 2) * T1, max(T1, T2))

        @pl.when(j == 0)
        def _():
            C1(i).start()

        @pl.when((j == 0) & (i >= 1))
        def _():
            core2(i - 1)

        @pl.when(j == 1)
        def _():
            phase1(i)
            count_step(i)

        @pl.when(j == 2)
        def _():
            C2(i).start()

        @pl.when((j == 2) & (i >= 1))
        def _():
            phase2(i - 1)

        @pl.when((j == 3) & (i >= 2))
        def _():
            phase3(i - 2)

    core2(Z - 1)
    phase2(Z - 1)
    phase3(Z - 2)
    phase3(Z - 1)
    cf = cZ[0:1, :]
    for z in range(1, Z):
        ZCc(z).wait_recv()
        cf = cf + cZr[z - 1, z:z + 1, :]
    cout_ref[...] = cf
    spread = jnp.broadcast_to(jnp.maximum(cf, 1.0), (kpd, kpd))
    eye = lax.broadcasted_iota(jnp.int32, (kpd, kpd), 0) == lax.broadcasted_iota(jnp.int32, (kpd, kpd), 1)
    col = jnp.sum(jnp.where(eye, spread, 0.0), axis=1, keepdims=True)
    tot = tab[4 * Z - 1, D * hb:(D + 2) * hb]
    for i in range(Z - 1):
        ZC(i, Z - 1 - i).wait_recv()
        tot = tot + rZ[i]
    out_ref[...] = tot / col

    cc.wait_send()
    for d in range(1, D):
        DC(d).wait_send()
    XC().wait_send()
    for z in range(1, Z):
        ZCc(z).wait_send()
        ZC(Z - 1 - z, z).wait_send()

    @pl.loop(0, Z)
    def _(i):
        C1(i).wait_send()
        C2(i).wait_send()
        for d in range(1, D):
            A1(i, d).wait_send()
            B2(i, d).wait_send()
        B1(i).wait_send()
        A2(i).wait_send()


def per_device(facts, row_owner, key_offset):
    n_dom, n_rep = lax.axis_size("dom"), lax.axis_size("rep")
    rows, M = facts.shape
    D, Z = n_dom // 2, n_rep // 2
    kpd = KEYS // (n_dom * n_rep)
    hb = kpd // 2
    T1, T2 = (3 * D - 2) * hb, (D + 2) * hb
    chunk = min(1024, rows)

    def vm(*shape, dtype=F32):
        return pltpu.VMEM(shape, dtype)

    def dma(*shape):
        return [pltpu.SemaphoreType.DMA(shape)] * 2 if shape else [pltpu.SemaphoreType.DMA] * 2

    scratch = [
        vm(1, rows, dtype=jnp.int32), vm(1, rows, dtype=jnp.int32), vm(1, rows, dtype=jnp.int32),
        vm(rows, M), vm(rows, M, dtype=BF16), vm(rows, M, dtype=BF16),
        vm(4 * Z, max(T1, T2), M), vm(Z, T1, M), vm(Z, T2, M),
        vm(Z, D - 1, 2 * hb, M), vm(Z, D * hb, M), vm(Z, hb, M), vm(Z, D - 1, hb, M), vm(Z - 1, 2 * hb, M),
        vm(D, 2 * Z, kpd), vm(D, 2 * Z, kpd), vm(D, 2 * Z, kpd), vm(D - 1, 2 * Z, kpd),
        vm(2 * Z, kpd), vm(2 * Z, kpd), vm(Z, kpd), vm(Z - 1, Z, kpd),
        pltpu.SemaphoreType.DMA((rows // chunk,)), pltpu.SemaphoreType.DMA((2,)),
        *dma(Z), *dma(Z), *dma(Z, D - 1), *dma(Z), *dma(Z), *dma(Z, D - 1), *dma(Z - 1),
        *dma(), *dma(D - 1), *dma(), *dma(Z - 1),
    ]
    vmem = pl.BlockSpec(memory_space=pltpu.VMEM)
    means, counts = pl.pallas_call(
        functools.partial(kernel, D, Z, hb, rows, M, chunk),
        out_shape=(jax.ShapeDtypeStruct((kpd, M), F32), jax.ShapeDtypeStruct((1, kpd), F32)),
        in_specs=[pl.BlockSpec(memory_space=pl.ANY)] * 3,
        out_specs=(vmem, vmem),
        scratch_shapes=scratch,
        compiler_params=pltpu.CompilerParams(
            collective_id=0, has_side_effects=True, vmem_limit_bytes=50 * 1024 * 1024
        ),
    )(row_owner.reshape(1, rows), key_offset.reshape(1, rows), facts)
    return means, counts.reshape(kpd)


def solution(mesh):
    placed = (P(("dom", "rep"), None), P(("dom", "rep"), None), P(("dom", "rep")))
    return jax.shard_map(
        per_device,
        mesh=mesh,
        in_specs=placed,
        out_specs=(P(("dom", "rep"), None), P(("dom", "rep"))),
        check_vma=False,
    )
```

time: 50.4 us -> 40.8 us (0.81)
  Pallas kernels: 46.8 us -> 37.2 us
  other arithmetic: 1.52 us -> 0 us
  local copies, waits for them, and re-layouts: 1.17 us -> 2.6 us
    pallas_call x1, Pallas kernels: 46.8 us -> 37.2 us  [per_device(): pl.pallas_call(functools.partial(kernel, D, Z, hb, rows, M, chunk), out_s...]
    unnamed x2 -> x6, local copies, waits for them, and re-layouts: 1.17 us -> 2.6 us
    add x1 -> x0, other arithmetic: 0.77 us -> none  [per_device(): crow = ((dc * D + d) * 2 + x) * Z + z]
    and x1 -> x0, other arithmetic: 0.74 us -> none  [per_device(): dc, d = (rel & 1, rel >> 1)]
where the time goes in v2:
time: 40.8 us; the launch traced here: 40.4 us
  Pallas kernels  37.2 us (91%)
  local copies, waits for them, and re-layouts  2.6 us (6%)
  between operations  0.65 us (2%)
    pallas_call x1, Pallas kernels, per_device(): pl.pallas_call(functools.partial(kernel, D, Z, hb, rows, M, chunk), out_s...  37.2 us
    unnamed x6, local copies, waits for them, and re-layouts  2.6 us

profile of v2, /device:TPU:0, one launch (start us, length us, event | category | flops | bytes accessed | tf_op | source)
XLA Modules:
  0.0 40.4 jit_solution(13503178145475038877)
XLA Ops:
  0.6 0.0 copy-start
  0.6 0.7 %copy-done = s32[4096,1]{0,1:T(1,128)S(1)} copy-done((s32[4096,1]{0,1:T(1,128)S(1)}, s32[4096,1]{0,1:T(1,128)}, u32[]{:S(2)}) %copy-start) | copy-done | bytes 16408
  1.3 0.0 copy-start.1
  1.4 0.7 %copy-done.1 = s32[4096]{0:T(1024)S(1)} copy-done((s32[4096]{0:T(1024)S(1)}, s32[4096]{0:T(1024)}, u32[]{:S(2)}) %copy-start.1) | copy-done | bytes 16408
  2.1 37.2 %shard_map.50 = (f32[128,256]{1,0:T(8,128)S(1)}, f32[1,128]{1,0:T(1,128)S(1)}) custom-call(s32[1,4096]{1,0:T(1,128)S(1)} %bitcast.3, s32[1,4096]{1,0:T(1,128)S(1)} %bitcast.4, f32[4096,256]{1,0:T(8,128)} %facts_ref.1), custom_call_target="tpu_custom_call" | custom-call | tf_op jit(solution)/shard_map/pallas_call | solution.py:310
  39.3 0.7 %copy.7 = f32[128,256]{1,0:T(8,128)} copy(f32[128,256]{1,0:T(8,128)S(1)} %get-tuple-element.8) | data formatting | bytes 262144
  39.9 0.5 %copy.8 = f32[128]{0:T(128)} copy(f32[128]{0:T(128)S(1)} %bitcast.5) | data formatting | bytes 1024
Async XLA Ops:
  0.6 0.7 %copy-start = (s32[4096,1]{0,1:T(1,128)S(1)}, s32[4096,1]{0,1:T(1,128)}, u32[]{:S(2)}) copy-start(s32[4096,1]{0,1:T(1,128)} %param.4) | copy-start | bytes 49156
  1.3 0.7 %copy-start.1 = (s32[4096]{0:T(1024)S(1)}, s32[4096]{0:T(1024)}, u32[]{:S(2)}) copy-start(s32[4096]{0:T(1024)} %param.5) | copy-start | bytes 49156
